TPU v7x, 32 devices: a whole 2x2x4 slice. The times are simulated.
32 devices in a mesh: dp: 16 (over z, x, core), tensor: 2 (over y).
Axes of the slice: x: 2, y: 2, z: 4, core: 2. Of those that a mesh axis runs over, the one named last changes fastest.
Arguments:
- drafter_hidden: bfloat16 [2, 2048, 4096], P(None, 'dp', 'tensor'), may hold values from -2000 to 2000
- norm_gain: bfloat16 [4096], P('tensor'), may hold values from 0.5 to 1.5
- head_weight: bfloat16 [4096, 8192], P('tensor', 'dp'), may hold values from -24 to 24
- labels: int32 [2048], P('dp'), may hold values from 0 to 8191
- loss_mask: int32 [2048], P('dp'), may hold values 0 or 1
- offsets: int32 [2], replicated, may hold values from 1 to 4
Outputs:
- draft_loss: float32 [], replicated
- head_grad: float32 [4096, 8192], P('tensor', 'dp')
All inputs are finite; a program needn't handle non-finite values. No bound on the sum of `loss_mask` on one device may be relied on, other than what follows from the above.
Results may differ from a plain program's by a relative error of at most 0.0048.
Values may be sent and summed in bfloat16 or wider, within the bound.
A program may use at most 128 MiB of HBM per device.

v0:
```python
import jax
import jax.numpy as jnp
from jax import lax
from jax.sharding import PartitionSpec as P

D = 4096
WINDOW = 512


epsilon = 1e-05
step_decay = 0.8


def combined_all(part, axis, combine):
    gathered = jax.tree.map(lambda a: lax.all_gather(a, axis), part)

    def take(source):
        return jax.tree.map(lambda a: lax.dynamic_index_in_dim(a, source, 0, False), gathered)

    return lax.fori_loop(
        1, lax.axis_size(axis), lambda source, state: combine(state, take(source)), take(0)
    )


def local(drafter_hidden, norm_gain, head_weight, labels, loss_mask, offsets):
    step_count, local_tokens, width_part = drafter_hidden.shape
    vocab_part = head_weight.shape[1]
    data_ways = lax.axis_size("dp")
    tensor_ways = lax.axis_size("tensor")
    data_rank = lax.axis_index("dp")
    tensor_rank = lax.axis_index("tensor")
    all_tokens = local_tokens * data_ways
    label_all, mask_all = (
        lax.all_gather(labels, "dp", axis=0, tiled=True),
        lax.all_gather(loss_mask, "dp", axis=0, tiled=True),
    )
    hidden_wide = drafter_hidden.astype(jnp.float32)
    squares = lax.psum(jnp.sum(hidden_wide * hidden_wide, axis=-1), "tensor")
    inverse = lax.rsqrt(squares / D + epsilon)
    normed = (hidden_wide * inverse[:, :, None] * norm_gain.astype(jnp.float32)).astype(
        jnp.bfloat16
    )
    gathered = lax.all_gather(normed, "dp", axis=1, tiled=True)
    rows_here = all_tokens // tensor_ways
    product = jnp.einsum("srd,dv->rsv", gathered, head_weight, preferred_element_type=jnp.float32)
    summed = lax.psum_scatter(
        product.reshape(lax.axis_size("tensor") * rows_here, step_count * vocab_part),
        "tensor",
        scatter_dimension=0,
        tiled=True,
    )
    logits = summed.reshape(rows_here, step_count, vocab_part).transpose(1, 0, 2)
    positions = tensor_rank * rows_here + jnp.arange(rows_here, dtype=jnp.int32)
    everywhere = jnp.arange(all_tokens, dtype=jnp.int32)
    label_list = []
    weight_list = []
    count_list = []
    for step_at in range(step_count):
        moved_by = offsets[step_at]
        inside = positions % WINDOW + moved_by < WINDOW
        clamped = jnp.minimum(positions + moved_by, all_tokens - 1)
        label_list.append(label_all[clamped])
        weight_list.append(jnp.where(inside, mask_all[clamped], 0).astype(jnp.float32))
        inside_all = everywhere % WINDOW + moved_by < WINDOW
        clamped_all = jnp.minimum(everywhere + moved_by, all_tokens - 1)
        count_list.append(
            jnp.sum(jnp.where(inside_all, mask_all[clamped_all], 0).astype(jnp.float32))
        )
    row_label = jnp.stack(label_list)
    row_weight = jnp.stack(weight_list)
    counted = jnp.stack(count_list)
    factors = step_decay ** jnp.arange(step_count, dtype=jnp.float32)
    columns = data_rank * vocab_part + jnp.arange(vocab_part, dtype=jnp.int32)
    hitting = columns[None, None, :] == row_label[:, :, None]
    local_top = jnp.max(logits, axis=-1)
    label_part = jnp.sum(jnp.where(hitting, logits, 0.0), axis=-1)
    local_total = jnp.sum(jnp.exp(logits - local_top[:, :, None]), axis=-1)

    def combine(earlier, latter):
        highest = jnp.maximum(earlier[0], latter[0])
        joined = earlier[1] * jnp.exp(earlier[0] - highest) + latter[1] * jnp.exp(
            latter[0] - highest
        )
        return (highest, joined, earlier[2] + latter[2])

    row_top, row_total, label_logit = combined_all(
        (local_top, local_total, label_part), "dp", combine
    )
    log_total = row_top + jnp.log(row_total)
    numerator = lax.psum(jnp.sum(row_weight * (log_total - label_logit), axis=-1), "tensor")
    loss_total = jnp.sum(factors * numerator / counted)
    softmax = jnp.exp(logits - log_total[:, :, None])
    slopes = (
        factors[:, None, None] * row_weight[:, :, None] * (softmax - hitting.astype(jnp.float32))
    ).astype(jnp.bfloat16)
    gradient = jnp.einsum(
        "srd,srv->dv",
        gathered,
        lax.all_gather(slopes, "tensor", axis=1, tiled=True),
        preferred_element_type=jnp.float32,
    )
    return (loss_total, gradient)


def solution(mesh):
    return jax.shard_map(
        local,
        mesh=mesh,
        in_specs=(P(None, "dp", "tensor"), P("tensor"), P("tensor", "dp"), P("dp"), P("dp"), P()),
        out_specs=(P(), P("tensor", "dp")),
        check_vma=False,
    )
```

profile of v0, /device:TPU:0, one launch (start us, length us, event | category | flops | bytes accessed | tf_op | source)
XLA Modules:
  0.0 406.5 jit_solution(12078184835807543823)
XLA Ops:
  7.2 0.0 copy-start
  7.2 0.0 all-gather.11.cloned.1.call-start
  7.2 0.8 convert_element_type.48
  8.1 1.5 fusion.9
  9.6 5.9 %psum.14 = f32[2,128]{1,0:T(2,128)S(1)} all-reduce(f32[2,128]{1,0:T(2,128)S(1)} %fusion.9), channel_id=1, replica_groups=mesh['dp'=16,'tensor'=2] {'tensor'}, use_global_device_ids=true, to_apply=%region_1.0 | all-reduce | flops 256 | bytes 2048 | tf_op jit(solution)/shard_map/psum | solution.py:38
  15.5 2.5 fusion.11
  18.0 0.0 all-gather.11.cloned.1.call-update
  18.0 0.0 reduce-scatter.2.cloned.1.call-start
  18.0 128.3 %all-gather.11.cloned.1.call-done = bf16[2,2048,2048]{2,1,0:T(8,128)(2,1)} async-done(((bf16[2,128,2048]{2,1,0:T(8,128)(2,1)}), bf16[2,2048,2048]{2,1,0:T(8,128)(2,1)}) %all-gather.11.cloned.1.call-update) | async-done | bytes 16777232 | tf_op jit(solution)/shard_map/all_gather | solution.py:43
  146.4 0.0 copy-done
  146.4 14.5 %fusion.12 = f32[2,2048,512]{1,2,0:T(8,128)} fusion(bf16[2,2048,2048]{2,1,0:T(8,128)(2,1)} %all-gather.11.cloned.1.call-done, bf16[2048,512]{1,0:T(8,128)(2,1)S(1)} %copy-done), kind=kOutput, calls=%fused_computation.30 | convolution fusion | flops 8589934592 | bytes 27262976 | tf_op jit(solution)/shard_map/srd,dv->rsv/dot_general | solution.py:45
  160.9 0.0 reduce-scatter.2.cloned.1.call-update
  160.9 0.0 all-gather.13.cloned.1.call-start
  161.0 0.6 copy-done.3
  161.5 18.4 %all-gather.6 = s32[16,1,128]{2,1,0:T(1,128)S(1)} all-gather(s32[1,1,128]{2,1,0:T(1,128)S(1)} %bitcast.85), channel_id=1, replica_groups=mesh['dp'=16,'tensor'=2] {'dp'}, dimensions={0}, use_global_device_ids=true | all-gather | bytes 8704 | tf_op jit(solution)/shard_map/all_gather | solution.py:34
  180.0 0.0 copy-done.2
  180.0 0.6 fusion.21
  180.6 1.3 compare_select_fusion.3
  182.0 0.0 copy-start.4
  182.0 6.2 %gather_fusion.3 = s32[1024]{0:T(1024)S(1)} fusion(s32[2048]{0:T(1024)S(1)} %bitcast.70, s32[1024]{0:T(1024)S(1)} %broadcast_clamp_fusion.2), kind=kCustom, calls=%fused_computation.3 | custom fusion | bytes 12288 | tf_op jit(solution)/shard_map/gather | solution.py:62
  188.2 6.2 %gather_fusion.2 = s32[1024]{0:T(1024)S(1)} fusion(s32[2048]{0:T(1024)S(1)} %bitcast.71, s32[1024]{0:T(1024)S(1)} %broadcast_clamp_fusion.3), kind=kCustom, calls=%fused_computation.2 | custom fusion | bytes 12288 | tf_op jit(solution)/shard_map/gather | solution.py:62
  194.3 0.0 copy-done.4
  194.3 17.8 %all-gather.3 = s32[16,1,128]{2,1,0:T(1,128)S(1)} all-gather(s32[1,1,128]{2,1,0:T(1,128)S(1)} %bitcast.86), channel_id=1, replica_groups=mesh['dp'=16,'tensor'=2] {'dp'}, dimensions={0}, use_global_device_ids=true | all-gather | bytes 8704 | tf_op jit(solution)/shard_map/all_gather | solution.py:35
  212.1 6.1 %gather_fusion.1 = s32[1024]{0:T(1024)S(1)} fusion(s32[2048]{0:T(1024)S(1)} %bitcast.66, s32[1024]{0:T(1024)S(1)} %broadcast_clamp_fusion.2), kind=kCustom, calls=%fused_computation.1 | custom fusion | bytes 12288 | tf_op jit(solution)/shard_map/gather | solution.py:63
  218.3 6.2 %gather_fusion = s32[1024]{0:T(1024)S(1)} fusion(s32[2048]{0:T(1024)S(1)} %bitcast.67, s32[1024]{0:T(1024)S(1)} %broadcast_clamp_fusion.3), kind=kCustom, calls=%fused_computation | custom fusion | bytes 12288 | tf_op jit(solution)/shard_map/gather | solution.py:63
  224.5 0.7 fusion.18
  225.2 0.7 fusion.17
  225.8 32.7 %reduce-scatter.2.cloned.1.call-done = f32[1024,1024]{0,1:T(8,128)} async-done(((f32[2048,1024]{0,1:T(8,128)}), f32[1024,1024]{0,1:T(8,128)}) %reduce-scatter.2.cloned.1.call-update) | async-done | bytes 4194320 | tf_op jit(solution)/shard_map/reduce_scatter | solution.py:46
  258.5 5.4 %copy.14 = f32[1024,2,512]{2,0,1:T(8,128)} copy(f32[1024,2,512]{0,2,1:T(8,128)} %bitcast.73) | data formatting | bytes 8388608 | tf_op jit(solution)/shard_map/reshape | solution.py:52
  263.9 2.7 bitcast_reduce_fusion
  266.6 21.7 %all-gather.4 = f32[16,2,1024]{2,1,0:T(2,128)S(1)} all-gather(f32[1,2,1024]{2,1,0:T(2,128)S(1)} %bitcast.74), channel_id=2, replica_groups=mesh['dp'=16,'tensor'=2] {'dp'}, dimensions={0}, use_global_device_ids=true | all-gather | bytes 139264 | tf_op jit(solution)/shard_map/all_gather | solution.py:15
  288.3 1.7 fusion.2
  290.0 17.8 %all-gather.5 = f32[16,2,1024]{2,1,0:T(2,128)S(1)} all-gather(f32[1,2,1024]{2,1,0:T(2,128)S(1)} %bitcast.76), channel_id=3, replica_groups=mesh['dp'=16,'tensor'=2] {'dp'}, dimensions={0}, use_global_device_ids=true | all-gather | bytes 139264 | tf_op jit(solution)/shard_map/all_gather | solution.py:15
  307.8 19.1 %all-gather.7 = f32[16,2,1024]{2,1,0:T(2,128)S(1)} all-gather(f32[1,2,1024]{2,1,0:T(2,128)S(1)} %bitcast.75), channel_id=4, replica_groups=mesh['dp'=16,'tensor'=2] {'dp'}, dimensions={0}, use_global_device_ids=true | all-gather | bytes 139264 | tf_op jit(solution)/shard_map/all_gather | solution.py:15
  326.9 0.8 while.19
  327.7 0.1 multiply_reduce_fusion
  327.8 3.8 fusion.5
  331.7 0.0 all-gather.13.cloned.1.call-update
  331.7 0.7 compare_select_fusion.1
  332.4 11.8 %gather_fusion.5 = s32[2048]{0:T(1024)S(1)} fusion(s32[2048]{0:T(1024)S(1)} %bitcast.68, s32[2048]{0:T(1024)S(1)} %broadcast_clamp_fusion), kind=kCustom, calls=%fused_computation.5 | custom fusion | bytes 24576 | tf_op jit(solution)/shard_map/gather | solution.py:67
  344.2 0.7 compare_select_fusion.2
  344.9 11.8 %gather_fusion.4 = s32[2048]{0:T(1024)S(1)} fusion(s32[2048]{0:T(1024)S(1)} %bitcast.69, s32[2048]{0:T(1024)S(1)} %broadcast_clamp_fusion.1), kind=kCustom, calls=%fused_computation.4 | custom fusion | bytes 24576 | tf_op jit(solution)/shard_map/gather | solution.py:67
  356.7 1.3 convert_reduce_fusion
  357.9 1.3 convert_reduce_fusion.1
  359.2 5.3 %psum.15 = f32[2]{0:T(128)S(1)} all-reduce(f32[2]{0:T(128)S(1)} %get-tuple-element.201), channel_id=1, replica_groups=mesh['dp'=16,'tensor'=2] {'tensor'}, use_global_device_ids=true, to_apply=%region_9.10 | all-reduce | flops 2 | bytes 16 | tf_op jit(solution)/shard_map/psum | solution.py:90
  364.5 2.0 fusion.20
  366.5 18.5 %all-gather.13.cloned.1.call-done = bf16[2,2048,512]{2,1,0:T(8,128)(2,1)} async-done(((bf16[2,1024,512]{2,1,0:T(8,128)(2,1)}), bf16[2,2048,512]{2,1,0:T(8,128)(2,1)}) %all-gather.13.cloned.1.call-update) | async-done | bytes 4194320 | tf_op jit(solution)/shard_map/all_gather | solution.py:99
  385.0 14.9 %convolution_bitcast_fusion = f32[2048,512]{1,0:T(8,128)} fusion(bf16[2,2048,2048]{2,1,0:T(8,128)(2,1)} %all-gather.11.cloned.1.call-done, bf16[2,2048,512]{2,1,0:T(8,128)(2,1)} %all-gather.13.cloned.1.call-done), kind=kOutput, calls=%fused_computation.24 | convolution fusion | flops 8589934592 | bytes 25165824 | tf_op jit(solution)/shard_map/srd,srv->dv/dot_general | solution.py:96
  (30 shorter events, 0.6 us)
Async XLA Ops:
  7.2 139.2 %copy-start = (bf16[2048,512]{1,0:T(8,128)(2,1)S(1)}, bf16[2048,512]{1,0:T(8,128)(2,1)}, u32[]{:S(2)}) copy-start(bf16[2048,512]{1,0:T(8,128)(2,1)} %param.10) | copy-start | bytes 6291460
  7.2 139.2 %all-gather.11.cloned.1.call-start = ((), (), s32[]{:S(2)}) async-start(), calls=%async_computation.1 | async-start | bytes 17825792 | tf_op jit(solution)/shard_map/all_gather | solution.py:43
  18.0 240.5 %reduce-scatter.2.cloned.1.call-start = ((), (), s32[]{:S(2)}) async-start(), calls=%async_computation.2 | async-start | bytes 12582912 | tf_op jit(solution)/shard_map/reduce_scatter | solution.py:46
  160.9 0.7 copy-start.3
  160.9 19.1 %copy-start.2 = (s32[2]{0:T(128)S(1)}, s32[2]{0:T(128)}, u32[]{:S(2)}) copy-start(s32[2]{0:T(128)} %param.13) | copy-start | bytes 28
  160.9 224.1 %all-gather.13.cloned.1.call-start = ((), (), s32[]{:S(2)}) async-start(), calls=%async_computation.3 | async-start | bytes 6291456 | tf_op jit(solution)/shard_map/all_gather | solution.py:99
  182.0 12.3 %copy-start.4 = (s32[128]{0:T(128)S(1)}, s32[128]{0:T(128)}, u32[]{:S(2)}) copy-start(s32[128]{0:T(128)} %param.12) | copy-start | bytes 1540
  263.9 24.4 %copy-start.1 = (f32[1024,2,512]{2,0,1:T(8,128)S(1)}, f32[1024,2,512]{2,0,1:T(8,128)}, u32[]{:S(2)}) copy-start(f32[1024,2,512]{2,0,1:T(8,128)} %copy.14) | copy-start | bytes 12582916
Sparse Core Ops, SparseCore 0:
  18.1 128.2 all-gather.10
  161.0 97.4 reduce-scatter.1
  331.8 53.1 all-gather.12
where the time goes:
time: 407 us; the launch traced here: 406 us
  waiting for transfers between devices  180 us (44%)
  blocking collectives  106 us (26%)
  local copies, waits for them, and re-layouts  54.8 us (13%)
  matrix products  29.4 us (7%)
  other arithmetic  22.4 us (6%)
  between operations  13.9 us (3%)
    all_gather x1, waiting for transfers between devices, local(): gathered = lax.all_gather(normed, 'dp', axis=1, tiled=True)  128 us
    all_gather x3, blocking collectives, combined_all(): gathered = jax.tree.map(lambda a: lax.all_gather(a, axis), part)  58.6 us
    reduce_scatter x1, waiting for transfers between devices, local(): lax.psum_scatter(product.reshape(lax.axis_size('tensor') * rows_here, ste...  32.7 us
    gather x2, local copies, waits for them, and re-layouts, local(): mask_all[clamped_all]  23.6 us
    all_gather x1, waiting for transfers between devices, local(): lax.all_gather(slopes, 'tensor', axis=1, tiled=True)  18.5 us
    all_gather x1, blocking collectives, local(): lax.all_gather(labels, 'dp', axis=0, tiled=True)  18.4 us
    all_gather x1, blocking collectives, local(): lax.all_gather(loss_mask, 'dp', axis=0, tiled=True)  17.8 us
    dot_general x1, matrix products, local(): jnp.einsum('srd,srv->dv', gathered, lax.all_gather(slopes, 'tensor', axis...  14.9 us
  transfers between devices with their start and end apart: 3, of which 3 were waited for; matrix products, arithmetic and copies ran while one was open for 14% of the time, Pallas kernels for 0%

commit v1 on v0

v1 whole, which is shorter than its diff:
```python
import functools

import jax
import jax.numpy as jnp
from jax import lax
from jax.experimental import pallas as pl
from jax.experimental.pallas import tpu as pltpu
from jax.sharding import PartitionSpec as P

WINDOW = 512
MAXOFF = 4

epsilon = 1e-05
step_decay = 0.8
MESH = pl.DeviceIdType.MESH


def spread_kernel(axes, sizes, *refs):
    count = len(axes)
    sources, targets = refs[:count], refs[count : 2 * count]
    held, sems = refs[2 * count : 3 * count], refs[3 * count :]
    barrier = pltpu.get_barrier_semaphore()
    peers = 0
    for axis, size in dict(zip(axes, sizes)).items():
        me = lax.axis_index(axis)
        for j in range(1, size):
            pl.semaphore_signal(
                barrier, inc=1, device_id={axis: lax.rem(me + j, size)}, device_id_type=MESH
            )
            peers += 1
    pl.semaphore_wait(barrier, peers)
    copies = []
    for k in range(count):
        me = lax.axis_index(axes[k])
        for j in range(1, sizes[k]):
            copy = pltpu.make_async_remote_copy(
                src_ref=sources[k],
                dst_ref=held[k].at[me],
                send_sem=sems[2 * k].at[j],
                recv_sem=sems[2 * k + 1].at[j],
                device_id={axes[k]: lax.rem(me + j, sizes[k])},
                device_id_type=MESH,
            )
            copy.start()
            copies.append(copy)
    for k in range(count):
        held[k][lax.axis_index(axes[k])] = sources[k][...]
    for copy in copies:
        copy.wait()
    for k in range(count):
        targets[k][...] = held[k][...]


def spread(pairs, identity):
    arrays = [a for a, _ in pairs]
    axes = [axis for _, axis in pairs]
    sizes = [lax.axis_size(axis) for axis in axes]
    shapes = [(size, *a.shape) for a, size in zip(arrays, sizes)]
    vmem = pl.BlockSpec(memory_space=pltpu.VMEM)
    sems = []
    for size in sizes:
        sems += [pltpu.SemaphoreType.DMA((size,))] * 2
    return pl.pallas_call(
        functools.partial(spread_kernel, axes, sizes),
        out_shape=[jax.ShapeDtypeStruct(s, a.dtype) for s, a in zip(shapes, arrays)],
        in_specs=[vmem] * len(arrays),
        out_specs=[vmem] * len(arrays),
        scratch_shapes=[pltpu.VMEM(s, a.dtype) for s, a in zip(shapes, arrays)] + sems,
        compiler_params=pltpu.CompilerParams(collective_id=identity, has_side_effects=True),
        name=f"spread{identity}",
    )(*arrays)


def logits_kernel(
    n, ways, normed, weight, gathered, logits, held, part, landed,
    send, recv, part_send, part_recv, out_sem, own_sem,
):
    steps, rows, vocab = part.shape[1:]
    mine = rows // ways
    line = n // 4
    me, rank = lax.axis_index("dp"), lax.axis_index("tensor")
    c, x, z = lax.rem(me, 2), lax.rem(me // 2, 2), me // 4
    sibling, other = 1 - c, 1 - x

    def at(z_, x_, c_):
        return (z_ * 2 + x_) * 2 + c_

    own = pltpu.make_async_copy(normed, held.at[me], own_sem)
    own.start()
    barrier = pltpu.get_barrier_semaphore()

    def greet(device):
        pl.semaphore_signal(barrier, inc=1, device_id=device, device_id_type=MESH)

    @pl.when(z > 0)
    def _():
        greet({"dp": at(z - 1, x, c)})

    @pl.when(z < line - 1)
    def _():
        greet({"dp": at(z + 1, x, c)})

    greet({"dp": at(z, other, c)})
    greet({"dp": at(z, x, sibling)})
    for j in range(1, ways):
        greet({"tensor": lax.rem(rank + j, ways)})
    chips = jnp.where(z > 0, 1, 0) + jnp.where(z < line - 1, 1, 0)
    pl.semaphore_wait(barrier, chips + 1 + ways)
    own.wait()

    def block_copy(kind, b, s, target):
        return pltpu.make_async_remote_copy(
            src_ref=held.at[b, s],
            dst_ref=held.at[b, s],
            send_sem=send.at[kind, b, s],
            recv_sem=recv.at[b, s],
            device_id={"dp": target},
            device_id_type=MESH,
        )

    def ups(b, s):
        return block_copy(0, b, s, at(z + 1, x, c))

    def downs(b, s):
        return block_copy(1, b, s, at(z - 1, x, c))

    def across(b, s):
        return block_copy(2, b, s, at(z, other, c))

    def beside(b, s):
        return block_copy(3, b, s, at(z, x, sibling))

    def part_copy(j, b, s):
        peer = lax.rem(rank + j, ways)
        return pltpu.make_async_remote_copy(
            src_ref=part.at[b, s, pl.ds(pl.multiple_of(peer * mine, mine), mine)],
            dst_ref=landed.at[j - 1, b, s],
            send_sem=part_send.at[j - 1, b, s],
            recv_sem=part_recv.at[j - 1, b, s],
            device_id={"tensor": peer},
            device_id_type=MESH,
        )

    def out_copy(b, s):
        return pltpu.make_async_copy(held.at[b, s], gathered.at[b, s], out_sem.at[b, s])

    def inside(zz):
        return jnp.logical_and(zz >= 0, zz < line)

    def stage(t, carry):
        k, s = t // steps, lax.rem(t, steps)
        for side in (0, 1):
            zz = z + k if side else z - k
            ok = jnp.logical_and(inside(zz), k > 0) if side else inside(zz)

            @pl.when(ok)
            def _(zz=zz):
                b = at(zz, x, c)

                @pl.when(k > 0)
                def _():
                    beside(b, s).wait_recv()

                @pl.when(jnp.logical_and(zz <= z, z < line - 1))
                def _():
                    ups(b, s).start()

                @pl.when(jnp.logical_and(zz >= z, z > 0))
                def _():
                    downs(b, s).start()

                across(b, s).start()
                beside(b, s).start()

        for side in (0, 1):
            zz = z + (k - 1) if side else z - (k - 1)
            ok = jnp.logical_and(inside(zz), k > side)

            @pl.when(ok)
            def _(zz=zz):
                b = at(zz, other, c)
                beside(b, s).wait_recv()
                beside(b, s).start()

        def multiply(q, carry):
            core, kind, side = q // 4, lax.rem(q // 2, 2), lax.rem(q, 2)
            away = k - kind
            zz = z + away * (2 * side - 1)
            ok = jnp.logical_and(inside(zz), away >= side)

            @pl.when(ok)
            def _():
                b = at(zz, lax.rem(x + kind, 2), lax.rem(c + core, 2))

                @pl.when(core > 0)
                def _():
                    beside(b, s).wait_recv()

                out_copy(b, s).start()
                part[b, s] = jnp.dot(held[b, s], weight[...], preferred_element_type=jnp.float32)
                for j in range(1, ways):
                    part_copy(j, b, s).start()

            return carry

        return lax.fori_loop(0, 8, multiply, carry)

    lax.fori_loop(0, (line + 1) * steps, stage, 0)

    def finish(u, carry):
        b, s = u // steps, lax.rem(u, steps)
        cb, xb, zb = lax.rem(b, 2), lax.rem(b // 2, 2), b // 4
        column = jnp.logical_and(xb == x, cb == c)

        @pl.when(jnp.logical_and(column, jnp.logical_and(zb <= z, z < line - 1)))
        def _():
            ups(b, s).wait_send()

        @pl.when(jnp.logical_and(column, jnp.logical_and(zb >= z, z > 0)))
        def _():
            downs(b, s).wait_send()

        @pl.when(column)
        def _():
            across(b, s).wait_send()

        @pl.when(cb == c)
        def _():
            beside(b, s).wait_send()

        out_copy(b, s).wait()
        for j in range(1, ways):
            part_copy(j, b, s).wait_recv()
        total = part[b, s, pl.ds(pl.multiple_of(rank * mine, mine), mine)]
        for j in range(1, ways):
            total += landed[j - 1, b, s]
        logits[b, s] = total
        for j in range(1, ways):
            part_copy(j, b, s).wait_send()
        return carry

    lax.fori_loop(0, n * steps, finish, 0)


def gather_and_multiply(normed, weight):
    steps, rows, width = normed.shape
    vocab = weight.shape[1]
    n, ways = lax.axis_size("dp"), lax.axis_size("tensor")
    mine = rows // ways
    vmem = pl.BlockSpec(memory_space=pltpu.VMEM)
    hbm = pl.BlockSpec(memory_space=pl.ANY)
    dma = pltpu.SemaphoreType.DMA
    return pl.pallas_call(
        functools.partial(logits_kernel, n, ways),
        out_shape=[
            jax.ShapeDtypeStruct((n, steps, rows, width), jnp.bfloat16),
            jax.ShapeDtypeStruct((n, steps, mine, vocab), jnp.float32),
        ],
        in_specs=[hbm, vmem],
        out_specs=[hbm, vmem],
        scratch_shapes=[
            pltpu.VMEM((n, steps, rows, width), jnp.bfloat16),
            pltpu.VMEM((n, steps, rows, vocab), jnp.float32),
            pltpu.VMEM((ways - 1, n, steps, mine, vocab), jnp.float32),
            dma((4, n, steps)),
            dma((n, steps)),
            dma((ways - 1, n, steps)),
            dma((ways - 1, n, steps)),
            dma((n, steps)),
            dma,
        ],
        compiler_params=pltpu.CompilerParams(
            collective_id=7, has_side_effects=True, vmem_limit_bytes=60 * 1024 * 1024
        ),
        name="gather_and_multiply",
    )(normed, weight)


def local(drafter_hidden, norm_gain, head_weight, labels, loss_mask, offsets):
    step_count, local_tokens, width_part = drafter_hidden.shape
    vocab_part = head_weight.shape[1]
    data_ways = lax.axis_size("dp")
    tensor_ways = lax.axis_size("tensor")
    data_rank = lax.axis_index("dp")
    tensor_rank = lax.axis_index("tensor")
    all_tokens = local_tokens * data_ways
    rows_each = local_tokens // tensor_ways
    hidden_wide = drafter_hidden.astype(jnp.float32)
    squares_all, token_all = spread(
        [
            (jnp.sum(hidden_wide * hidden_wide, axis=-1), "tensor"),
            (jnp.stack([labels, loss_mask]), "dp"),
        ],
        5,
    )
    inverse = lax.rsqrt(jnp.sum(squares_all, axis=0) / (width_part * tensor_ways) + epsilon)
    normed = (hidden_wide * inverse[:, :, None] * norm_gain.astype(jnp.float32)).astype(
        jnp.bfloat16
    )
    gathered, logits = gather_and_multiply(normed, head_weight)

    everywhere = jnp.arange(all_tokens, dtype=jnp.int32)

    def moved(values, by):
        padded = jnp.concatenate([values, jnp.broadcast_to(values[-1:], (MAXOFF,))])
        result = padded[MAXOFF : MAXOFF + all_tokens]
        for far in range(1, MAXOFF):
            result = jnp.where(by == far, padded[far : far + all_tokens], result)
        return result

    def own_rows(values):
        grid = values.reshape(data_ways, local_tokens)
        return lax.dynamic_slice_in_dim(grid, tensor_rank * rows_each, rows_each, 1)

    label_flat = token_all[:, 0].reshape(all_tokens)
    mask_flat = token_all[:, 1].reshape(all_tokens)
    label_list, weight_list, count_list = [], [], []
    for step_at in range(step_count):
        by = offsets[step_at]
        inside = everywhere % WINDOW + by < WINDOW
        weights = jnp.where(inside, moved(mask_flat, by), 0).astype(jnp.float32)
        count_list.append(jnp.sum(weights))
        weight_list.append(own_rows(weights))
        label_list.append(own_rows(moved(label_flat, by)))
    row_label = jnp.stack(label_list, axis=1)
    row_weight = jnp.stack(weight_list, axis=1)
    counted = jnp.stack(count_list)
    factors = step_decay ** jnp.arange(step_count, dtype=jnp.float32)

    columns = data_rank * vocab_part + jnp.arange(vocab_part, dtype=jnp.int32)
    hitting = columns == row_label[..., None]
    local_top = jnp.max(logits, axis=-1)
    label_part = jnp.sum(jnp.where(hitting, logits, 0.0), axis=-1)
    local_lse = local_top + jnp.log(jnp.sum(jnp.exp(logits - local_top[..., None]), axis=-1))
    (lse_all,) = spread([(local_lse.reshape(-1, local_tokens), "dp")], 6)
    top = jnp.max(lse_all, axis=0)
    log_total = (top + jnp.log(jnp.sum(jnp.exp(lse_all - top), axis=0))).reshape(local_lse.shape)
    softmax = jnp.exp(logits - log_total[..., None])
    slopes = (
        factors[:, None, None] * row_weight[..., None] * (softmax - hitting.astype(jnp.float32))
    ).astype(jnp.bfloat16)

    parts = [slopes]
    for far in range(1, tensor_ways):
        parts.append(
            lax.ppermute(
                slopes, "tensor", [(i, (i + far) % tensor_ways) for i in range(tensor_ways)]
            )
        )
    ordered = [
        lax.select_n(
            jnp.broadcast_to((tensor_rank - place) % tensor_ways == 1, slopes.shape), *parts
        )
        if tensor_ways == 2
        else lax.dynamic_index_in_dim(
            jnp.stack(parts), (tensor_rank - place) % tensor_ways, 0, False
        )
        for place in range(tensor_ways)
    ]
    gradient = jnp.einsum(
        "nsrd,nsrv->dv",
        gathered,
        jnp.concatenate(ordered, axis=2),
        preferred_element_type=jnp.float32,
    )

    shared = jnp.where(data_rank == 0, log_total, 0.0) - label_part
    numerator = lax.psum(jnp.sum(row_weight * shared, axis=(0, 2)), ("dp", "tensor"))
    loss_total = jnp.sum(factors * numerator / counted)
    return (loss_total, gradient)


def solution(mesh):
    return jax.shard_map(
        local,
        mesh=mesh,
        in_specs=(P(None, "dp", "tensor"), P("tensor"), P("tensor", "dp"), P("dp"), P("dp"), P()),
        out_specs=(P(), P("tensor", "dp")),
        check_vma=False,
    )
```

time: 407 us -> 263 us (0.65)
  waiting for transfers between devices: 180 us -> 0.01 us
  Pallas kernels: 0 us -> 127 us
  local copies, waits for them, and re-layouts: 54.8 us -> 4.27 us
  blocking collectives: 106 us -> 81.3 us
  matrix products: 29.4 us -> 13.8 us
  between operations: 13.9 us -> 4.59 us
  other arithmetic: 22.4 us -> 30.6 us
    all_gather x2 -> x0, waiting for transfers between devices: 147 us -> none  [the longest x1 128 us: local(): gathered = lax.all_gather(normed, 'dp', axis=1, tiled=True)]
    pallas_call x0 -> x3, Pallas kernels: none -> 127 us  [the longest x1 106 us: gather_and_multiply(): pl.pallas_call(functools.partial(logits_kernel, n, ways), out_shape=[jax....]
    all_gather x5 -> x0, blocking collectives: 94.8 us -> none  [the longest x3 58.6 us: combined_all(): gathered = jax.tree.map(lambda a: lax.all_gather(a, axis), part)]
    psum x2 -> x1, blocking collectives: 11.2 us -> 81.3 us  [local(): lax.psum(jnp.sum(row_weight * shared, axis=(0, 2)), ('dp', 'tensor'))]
    gather x6 -> x0, local copies, waits for them, and re-layouts: 48.2 us -> none  [the longest x2 23.6 us: local(): mask_all[clamped_all]]
    reduce_scatter x1 -> x0, waiting for transfers between devices: 32.7 us -> none  [local(): lax.psum_scatter(product.reshape(lax.axis_size('tensor') * rows_here, ste...]
    dot_general x2 -> x1, matrix products: 29.4 us -> 13.8 us  [local(): jnp.einsum('nsrd,nsrv->dv', gathered, jnp.concatenate(ordered, axis=2), p...]
    reshape x1 -> x0, local copies, waits for them, and re-layouts: 5.36 us -> none  [local(): summed.reshape(rows_here, step_count, vocab_part).transpose(1, 0, 2)]
  transfers between devices with their start and end apart: 3 -> 1, of which waited for: 3 -> 0; matrix products, arithmetic and copies ran while one was open for 14% -> 1% of each run, Pallas kernels for 0% -> 0%
where the time goes in v1:
time: 263 us; the launch traced here: 262 us
  Pallas kernels  127 us (48%)
  blocking collectives  81.3 us (31%)
  other arithmetic  30.6 us (12%)
  matrix products  13.8 us (5%)
  between operations  4.59 us (2%)
  local copies, waits for them, and re-layouts  4.27 us (2%)
    pallas_call x1, Pallas kernels, gather_and_multiply(): pl.pallas_call(functools.partial(logits_kernel, n, ways), out_shape=[jax....  106 us
    psum x1, blocking collectives, local(): lax.psum(jnp.sum(row_weight * shared, axis=(0, 2)), ('dp', 'tensor'))  81.3 us
    pallas_call x2, Pallas kernels, spread(): pl.pallas_call(functools.partial(spread_kernel, axes, sizes), out_shape=[...  20.7 us
    dot_general x1, matrix products, local(): jnp.einsum('nsrd,nsrv->dv', gathered, jnp.concatenate(ordered, axis=2), p...  13.8 us
    select_n x1, other arithmetic, local(): lax.select_n(jnp.broadcast_to((tensor_rank - place) % tensor_ways == 1, s...  6.19 us
  transfers between devices with their start and end apart: 1, of which 0 were waited for; matrix products, arithmetic and copies ran while one was open for 1% of the time, Pallas kernels for 0%

profile of v1, /device:TPU:0, one launch (start us, length us, event | category | flops | bytes accessed | tf_op | source)
XLA Modules:
  0.0 261.9 jit_solution(1381588025866126477)
XLA Ops:
  0.6 1.4 fusion.23
  5.9 2.1 fusion.11.refs_0_
  8.0 0.7 convert_element_type.30
  8.7 1.2 pad_add_fusion.1.refs_1_
  9.9 10.7 %spread5.1 = (f32[2,2,128]{2,1,0:T(2,128)}, s32[16,2,128]{2,1,0:T(2,128)}) custom-call(f32[2,128]{1,0:T(2,128)} %fusion.11.refs_0_, s32[2,128]{1,0:T(2,128)} %pad_add_fusion.1.refs_1_), custom_call_target="tpu_custom_call" | custom-call | tf_op jit(solution)/shard_map/spread5/pallas_call | solution.py:63
  20.6 0.8 fusion.22
  21.4 0.7 slice.67
  22.1 0.6 slice.66
  22.7 0.7 reduce_sum.82
  23.4 0.8 select_bitcast_fusion.1
  24.2 2.6 %convert_reduce_fusion.1 = (f32[]{:T(128)}, s32[2048]{0:T(1024)S(1)}, f32[]{:T(128)}, s32[2048]{0:T(1024)S(1)}) fusion(s32[]{:T(128)} %bitcast, pred[]{:T(512)S(6)} %eq.54, pred[]{:T(512)S(6)} %eq.53, s32[2048]{0:T(1024)S(1)} %bitcast.40, s32[]{:T(128)} %bitcast.4, pred[]{:T(512)S(6)} %eq.52, pred[]{:T(512)S(6)} %eq.57, pred[]{:T(512)S(6)} %eq.56, ...), kind=kLoop, calls=%fused_computation.44 | loop fusion | flops 45054 | bytes 24602 | tf_op jit(solution)/shard_map/reduce_sum | solution.py:322
  26.8 0.1 constant_dynamic-slice_fusion.1
  26.9 1.4 fusion.16
  28.2 2.5 fusion.13.normed
  30.8 106.3 %gather_and_multiply.1 = (bf16[16,2,128,2048]{3,2,1,0:T(8,128)(2,1)}, f32[16,2,64,512]{3,2,1,0:T(8,128)}) custom-call(bf16[2,128,2048]{2,1,0:T(8,128)(2,1)} %fusion.13.normed, bf16[2048,512]{1,0:T(8,128)(2,1)} %weight.1), custom_call_target="tpu_custom_call" | custom-call | tf_op jit(solution)/shard_map/gather_and_multiply/pallas_call | solution.py:253
  137.1 2.5 reduce_max.18
  139.6 3.1 %exponential_reduce_fusion = (f32[16,2,64]{2,1,0:T(2,128)S(1)}, f32[16,2,64]{2,1,0:T(2,128)S(1)}) fusion(f32[16,2,64,512]{3,2,1,0:T(8,128)} %get-tuple-element.8, f32[16,2,64]{2,1,0:T(2,128)S(1)} %reduce_max.18, s32[16,2,64]{2,1,0:T(2,128)S(1)} %pad_add_fusion, s32[512]{0:T(512)S(1)} %iota_add_fusion), kind=kLoop, calls=%fused_computation.10 | loop fusion | flops 5238784 | bytes 4229120 | tf_op jit(solution)/shard_map/reduce_sum | solution.py:334
  142.8 0.7 add.111.refs_0_
  143.4 10.0 %spread6.1 = f32[16,16,128]{2,1,0:T(8,128)} custom-call(f32[16,128]{1,0:T(8,128)} %add.111.refs_0_), custom_call_target="tpu_custom_call" | custom-call | tf_op jit(solution)/shard_map/spread6/pallas_call | solution.py:63
  153.4 0.9 reduce_max.19
  154.4 0.9 exponential_reduce_fusion.1
  155.3 0.1 add.113
  155.4 0.1 broadcast_multiply_fusion
  155.6 2.8 %fusion.3 = bf16[16,2,64,512]{3,2,1,0:T(8,128)(2,1)S(1)} fusion(f32[16,2,64,512]{3,2,1,0:T(8,128)} %get-tuple-element.8, f32[16,2,64]{2,1,0:T(2,128)S(1)} %add.113, f32[16,2,64]{2,1,0:T(2,128)S(1)} %get-tuple-element.18, s32[16,2,64]{2,1,0:T(2,128)S(1)} %pad_add_fusion, s32[512]{0:T(512)S(1)} %iota_add_fusion), kind=kLoop, calls=%fused_computation.5 | loop fusion | flops 6291456 | bytes 6318080 | tf_op jit(solution)/shard_map/convert_element_type | solution.py:341
  158.4 0.3 collective-permute-start
  158.7 81.3 %psum.7 = f32[2]{0:T(128)S(1)} all-reduce(f32[2]{0:T(128)S(1)} %get-tuple-element.19), channel_id=1, replica_groups=mesh['dp'=16,'tensor'=2] {'dp','tensor'}, use_global_device_ids=true, to_apply=%region_8.9 | all-reduce | flops 2 | bytes 16 | tf_op jit(solution)/shard_map/psum | solution.py:368
  240.0 1.9 fusion.20
  241.9 0.0 collective-permute-done
  241.9 6.2 %broadcast_select_fusion.1 = (bf16[16,2,64,512]{3,2,1,0:T(8,128)(2,1)S(1)}, bf16[16,2,64,512]{3,2,1,0:T(8,128)(2,1)S(1)}) fusion(bf16[16,2,64,512]{3,2,1,0:T(8,128)(2,1)} %collective-permute-done, pred[]{:T(512)S(6)} %eq.62, pred[]{:T(512)S(6)} %eq.63, s32[16,2,64]{2,1,0:T(2,128)S(1)} %pad_add_fusion, s32[512]{0:T(512)S(1)} %iota_add_fusion, ...), kind=kLoop, calls=%fused_computation.18 | loop fusion | flops 8388608 | bytes 10512386 | tf_op jit(solution)/shard_map/select_n | solution.py:351
  248.1 13.8 %fusion.8 = f32[2048,512]{1,0:T(8,128)} fusion(bf16[16,2,128,2048]{3,2,1,0:T(8,128)(2,1)} %get-tuple-element.9, bf16[16,2,64,512]{3,2,1,0:T(8,128)(2,1)S(1)} %get-tuple-element.17, bf16[16,2,64,512]{3,2,1,0:T(8,128)(2,1)S(1)} %get-tuple-element.16), kind=kOutput, calls=%fused_computation.11 | convolution fusion | flops 8598323200 | bytes 25165824 | tf_op jit(solution)/shard_map/nsrd,nsrv->dv/dot_general | solution.py:360
  (7 shorter events, 0.1 us)
Async XLA Ops:
  158.4 83.5 %collective-permute-start = (bf16[16,2,64,512]{3,2,1,0:T(8,128)(2,1)S(1)}, bf16[16,2,64,512]{3,2,1,0:T(8,128)(2,1)}, u32[]{:S(2)}, u32[]{:S(2)}) collective-permute-start(bf16[16,2,64,512]{3,2,1,0:T(8,128)(2,1)S(1)} %fusion.3), channel_id=1, source_target_pairs={{0,1},{1,0},{2,3},{3,2},{4,5},{5,4},{6,7},{7,6},{8,9},{9,8},{10,11... | collective-permute-start | bytes 6291464 | tf_op jit(solution)/shard_map/ppermute | solution.py:346

commit v2 on v1

--- a/solution.py
+++ b/solution.py
@@ -72,9 +72,10 @@
 
 
 def logits_kernel(
-    n, ways, normed, weight, gathered, logits, held, part, landed,
-    send, recv, part_send, part_recv, out_sem, own_sem,
+    n, ways, normed, weight, *refs
 ):
+    gathered = refs[:ways]
+    logits, held, part, landed, send, recv, part_send, part_recv, out_sem, own_sem = refs[ways:]
     steps, rows, vocab = part.shape[1:]
     mine = rows // ways
     line = n // 4
@@ -141,8 +142,13 @@
             device_id_type=MESH,
         )
 
-    def out_copy(b, s):
-        return pltpu.make_async_copy(held.at[b, s], gathered.at[b, s], out_sem.at[b, s])
+    def out_copy(far, b, s):
+        owner = lax.rem(rank - far + ways, ways)
+        return pltpu.make_async_copy(
+            held.at[b, s, pl.ds(pl.multiple_of(owner * mine, mine), mine)],
+            gathered[far].at[b, s],
+            out_sem.at[far, b, s],
+        )
 
     def inside(zz):
         return jnp.logical_and(zz >= 0, zz < line)
@@ -196,7 +202,8 @@
                 def _():
                     beside(b, s).wait_recv()
 
-                out_copy(b, s).start()
+                for far in range(ways):
+                    out_copy(far, b, s).start()
                 part[b, s] = jnp.dot(held[b, s], weight[...], preferred_element_type=jnp.float32)
                 for j in range(1, ways):
                     part_copy(j, b, s).start()
@@ -228,7 +235,8 @@
         def _():
             beside(b, s).wait_send()
 
-        out_copy(b, s).wait()
+        for far in range(ways):
+            out_copy(far, b, s).wait()
         for j in range(1, ways):
             part_copy(j, b, s).wait_recv()
         total = part[b, s, pl.ds(pl.multiple_of(rank * mine, mine), mine)]
@@ -253,11 +261,11 @@
     return pl.pallas_call(
         functools.partial(logits_kernel, n, ways),
         out_shape=[
-            jax.ShapeDtypeStruct((n, steps, rows, width), jnp.bfloat16),
+            *[jax.ShapeDtypeStruct((n, steps, mine, width), jnp.bfloat16)] * ways,
             jax.ShapeDtypeStruct((n, steps, mine, vocab), jnp.float32),
         ],
         in_specs=[hbm, vmem],
-        out_specs=[hbm, vmem],
+        out_specs=[hbm] * ways + [vmem],
         scratch_shapes=[
             pltpu.VMEM((n, steps, rows, width), jnp.bfloat16),
             pltpu.VMEM((n, steps, rows, vocab), jnp.float32),
@@ -266,7 +274,7 @@
             dma((n, steps)),
             dma((ways - 1, n, steps)),
             dma((ways - 1, n, steps)),
-            dma((n, steps)),
+            dma((ways, n, steps)),
             dma,
         ],
         compiler_params=pltpu.CompilerParams(
@@ -297,7 +305,7 @@
     normed = (hidden_wide * inverse[:, :, None] * norm_gain.astype(jnp.float32)).astype(
         jnp.bfloat16
     )
-    gathered, logits = gather_and_multiply(normed, head_weight)
+    *gathered, logits = gather_and_multiply(normed, head_weight)
 
     everywhere = jnp.arange(all_tokens, dtype=jnp.int32)
 
@@ -332,7 +340,12 @@
     local_top = jnp.max(logits, axis=-1)
     label_part = jnp.sum(jnp.where(hitting, logits, 0.0), axis=-1)
     local_lse = local_top + jnp.log(jnp.sum(jnp.exp(logits - local_top[..., None]), axis=-1))
-    (lse_all,) = spread([(local_lse.reshape(-1, local_tokens), "dp")], 6)
+    label_sum = jnp.sum(row_weight * label_part, axis=(0, 2))
+    lse_rows = local_lse.reshape(-1, local_tokens)
+    label_rows = jnp.broadcast_to(label_sum[:, None], (step_count, local_tokens))
+    (spread_all,) = spread([(jnp.concatenate([lse_rows, label_rows]), "dp")], 6)
+    lse_all = spread_all[:, : lse_rows.shape[0]]
+    label_total = jnp.sum(spread_all[:, lse_rows.shape[0] :, 0], axis=0)
     top = jnp.max(lse_all, axis=0)
     log_total = (top + jnp.log(jnp.sum(jnp.exp(lse_all - top), axis=0))).reshape(local_lse.shape)
     softmax = jnp.exp(logits - log_total[..., None])
@@ -347,25 +360,16 @@
                 slopes, "tensor", [(i, (i + far) % tensor_ways) for i in range(tensor_ways)]
             )
         )
-    ordered = [
-        lax.select_n(
-            jnp.broadcast_to((tensor_rank - place) % tensor_ways == 1, slopes.shape), *parts
-        )
-        if tensor_ways == 2
-        else lax.dynamic_index_in_dim(
-            jnp.stack(parts), (tensor_rank - place) % tensor_ways, 0, False
-        )
-        for place in range(tensor_ways)
-    ]
-    gradient = jnp.einsum(
-        "nsrd,nsrv->dv",
-        gathered,
-        jnp.concatenate(ordered, axis=2),
-        preferred_element_type=jnp.float32,
-    )
-
-    shared = jnp.where(data_rank == 0, log_total, 0.0) - label_part
-    numerator = lax.psum(jnp.sum(row_weight * shared, axis=(0, 2)), ("dp", "tensor"))
+    gradient = sum(
+        jnp.einsum("nsrd,nsrv->dv", rows, part, preferred_element_type=jnp.float32)
+        for rows, part in zip(gathered, parts)
+    )
+
+    own_sum = jnp.sum(row_weight * log_total, axis=(0, 2)) - label_total
+    (sums_all,) = spread(
+        [(jnp.broadcast_to(own_sum[:, None], (step_count, local_tokens)), "tensor")], 8
+    )
+    numerator = jnp.sum(sums_all[:, :, 0], axis=0)
     loss_total = jnp.sum(factors * numerator / counted)
     return (loss_total, gradient)
 

time: 263 us -> 229 us (0.87)
  blocking collectives: 81.3 us -> 0 us
  Pallas kernels: 127 us -> 174 us
  matrix products: 13.8 us -> 17.5 us
  other arithmetic: 30.6 us -> 27.3 us
    psum x1 -> x0, blocking collectives: 81.3 us -> none  [local(): lax.psum(jnp.sum(row_weight * shared, axis=(0, 2)), ('dp', 'tensor'))]
    pallas_call x2 -> x3, Pallas kernels: 20.7 us -> 67.7 us  [spread(): pl.pallas_call(functools.partial(spread_kernel, axes, sizes), out_shape=[...]
    select_n x1 -> x0, other arithmetic: 6.19 us -> none  [local(): lax.select_n(jnp.broadcast_to((tensor_rank - place) % tensor_ways == 1, s...]
    dot_general x1 -> x2, matrix products: 13.8 us -> 17.5 us  [local(): jnp.einsum('nsrd,nsrv->dv', rows, part, preferred_element_type=jnp.float32)]
  transfers between devices with their start and end apart: 1 -> 1, of which waited for: 0 -> 0; matrix products, arithmetic and copies ran while one was open for 1% -> 5% of each run, Pallas kernels for 0% -> 20%
where the time goes in v2:
time: 229 us; the launch traced here: 228 us
  Pallas kernels  174 us (76%)
  other arithmetic  27.3 us (12%)
  matrix products  17.5 us (8%)
  between operations  4.54 us (2%)
  local copies, waits for them, and re-layouts  4.36 us (2%)
    pallas_call x1, Pallas kernels, gather_and_multiply(): pl.pallas_call(functools.partial(logits_kernel, n, ways), out_shape=[*[ja...  107 us
    pallas_call x3, Pallas kernels, spread(): pl.pallas_call(functools.partial(spread_kernel, axes, sizes), out_shape=[...  67.7 us
    dot_general x2, matrix products, local(): jnp.einsum('nsrd,nsrv->dv', rows, part, preferred_element_type=jnp.float32)  17.5 us
  transfers between devices with their start and end apart: 1, of which 0 were waited for; matrix products, arithmetic and copies ran while one was open for 5% of the time, Pallas kernels for 20%

profile of v2, /device:TPU:0, one launch (start us, length us, event | category | flops | bytes accessed | tf_op | source)
XLA Modules:
  0.0 228.3 jit_solution(12554543558364483176)
XLA Ops:
  0.6 1.3 fusion.15
  5.8 2.1 fusion.4.refs_0_
  7.9 1.2 pad_add_fusion.1.refs_1_
  9.1 10.7 %spread5.1 = (f32[2,2,128]{2,1,0:T(2,128)}, s32[16,2,128]{2,1,0:T(2,128)}) custom-call(f32[2,128]{1,0:T(2,128)} %fusion.4.refs_0_, s32[2,128]{1,0:T(2,128)} %pad_add_fusion.1.refs_1_), custom_call_target="tpu_custom_call" | custom-call | tf_op jit(solution)/shard_map/spread5/pallas_call | solution.py:63
  19.8 0.8 fusion.14
  20.6 0.6 slice.78
  21.2 0.7 slice.79
  21.9 2.7 %convert_reduce_fusion.1 = (f32[]{:T(128)}, s32[2048]{0:T(1024)S(1)}, f32[]{:T(128)}, s32[2048]{0:T(1024)S(1)}) fusion(s32[]{:T(128)} %bitcast, pred[]{:T(512)S(6)} %eq.42, pred[]{:T(512)S(6)} %eq.41, s32[2048]{0:T(1024)S(1)} %bitcast.49, s32[]{:T(128)} %bitcast.4, pred[]{:T(512)S(6)} %eq.40, pred[]{:T(512)S(6)} %eq.45, pred[]{:T(512)S(6)} %eq.44, ...), kind=kLoop, calls=%fused_computation.42 | loop fusion | flops 45054 | bytes 24602 | tf_op jit(solution)/shard_map/reduce_sum | solution.py:330
  24.6 0.8 select_bitcast_fusion.1
  25.3 0.7 convert_element_type.30
  26.0 0.7 reduce_sum.109
  26.7 2.5 %fusion.6.normed = bf16[2,128,2048]{2,1,0:T(8,128)(2,1)} fusion(bf16[2,128,2048]{2,1,0:T(8,128)(2,1)} %param.6, f32[2048]{0:T(1024)S(1)} %convert_element_type.30, f32[2,128]{1,0:T(2,128)S(1)} %add_rsqrt_fusion), kind=kLoop, calls=%fused_computation.12 | loop fusion | flops 2097152 | bytes 2106368 | tf_op jit(solution)/shard_map/convert_element_type | solution.py:305
  29.2 106.6 %gather_and_multiply.1 = (bf16[16,2,64,2048]{3,2,1,0:T(8,128)(2,1)}, bf16[16,2,64,2048]{3,2,1,0:T(8,128)(2,1)}, f32[16,2,64,512]{3,2,1,0:T(8,128)}) custom-call(bf16[2,128,2048]{2,1,0:T(8,128)(2,1)} %fusion.6.normed, bf16[2048,512]{1,0:T(8,128)(2,1)} %weight.1), custom_call_target="tpu_custom_call" | custom-call | tf_op jit(solution)/shard_map/gather_and_multiply/pallas_call | solution.py:261
  135.8 2.5 %reduce_max.18 = f32[16,2,64]{2,1,0:T(2,128)S(1)} reduce(f32[16,2,64,512]{3,2,1,0:T(8,128)} %get-tuple-element.9, f32[]{:T(128)} %constant.52.clone.1), dimensions={3}, to_apply=%region_2.3 | reduce | flops 1046528 | bytes 4202500 | tf_op jit(solution)/shard_map/reduce_max | solution.py:340
  138.4 0.1 constant_dynamic-slice_fusion.1
  138.5 1.3 fusion.9
  139.8 3.2 %fusion = (f32[16,2,64]{2,1,0:T(2,128)S(1)}, f32[16,2,64]{2,1,0:T(2,128)S(1)}) fusion(f32[16,2,64,512]{3,2,1,0:T(8,128)} %get-tuple-element.9, s32[16,2,64]{2,1,0:T(2,128)S(1)} %pad_add_fusion, s32[512]{0:T(512)S(1)} %iota_add_fusion, f32[16,2,64]{2,1,0:T(2,128)S(1)} %reduce_max.18), kind=kLoop, calls=%fused_computation.2 | loop fusion | flops 5238784 | bytes 4229120 | tf_op jit(solution)/shard_map/reduce_sum | solution.py:341
  143.1 0.1 add.104
  143.2 0.1 multiply_reduce_fusion.1
  143.3 0.1 pad.5.clone
  143.4 0.7 pad_maximum_fusion.1.refs_0_
  144.1 10.3 %spread6.1 = f32[16,18,128]{2,1,0:T(8,128)} custom-call(f32[18,128]{1,0:T(8,128)} %pad_maximum_fusion.1.refs_0_), custom_call_target="tpu_custom_call" | custom-call | tf_op jit(solution)/shard_map/spread6/pallas_call | solution.py:63
  154.4 0.9 slice_reduce_fusion
  155.3 0.9 exponential_reduce_fusion.1
  156.3 0.1 add.108
  156.3 0.1 broadcast_multiply_fusion
  156.5 2.9 %fusion.3 = bf16[16,2,64,512]{3,2,1,0:T(8,128)(2,1)S(1)} fusion(f32[16,2,64,512]{3,2,1,0:T(8,128)} %get-tuple-element.9, f32[16,2,64]{2,1,0:T(2,128)S(1)} %add.108, f32[16,2,64]{2,1,0:T(2,128)S(1)} %get-tuple-element.18, s32[16,2,64]{2,1,0:T(2,128)S(1)} %pad_add_fusion, s32[512]{0:T(512)S(1)} %iota_add_fusion), kind=kLoop, calls=%fused_computation.5 | loop fusion | flops 6291456 | bytes 6318080 | tf_op jit(solution)/shard_map/convert_element_type | solution.py:354
  159.3 0.3 collective-permute-start
  159.7 1.0 slice_reduce_fusion.1
  160.7 0.6 broadcast_in_dim.18.refs_0_
  161.3 46.7 %spread8.1 = f32[2,2,128]{2,1,0:T(2,128)} custom-call(f32[2,128]{1,0:T(2,128)} %broadcast_in_dim.18.refs_0_), custom_call_target="tpu_custom_call" | custom-call | tf_op jit(solution)/shard_map/spread8/pallas_call | solution.py:63
  208.0 0.8 slice_reduce_fusion.2
  208.8 2.0 fusion.13
  210.8 6.9 %fusion.16 = f32[2048,512,1,1]{1,0,3,2:T(8,128)S(1)} fusion(bf16[16,2,64,2048]{3,2,1,0:T(8,128)(2,1)} %get-tuple-element.10, bf16[16,2,64,512]{3,2,1,0:T(8,128)(2,1)S(1)} %fusion.3), kind=kOutput, calls=%fused_computation.66 | convolution fusion | flops 4294967296 | bytes 14680064 | tf_op jit(solution)/shard_map/nsrd,nsrv->dv/dot_general | solution.py:364
  217.8 0.0 collective-permute-done
  217.8 10.6 %bitcast_add_fusion = f32[2048,512]{1,0:T(8,128)} fusion(f32[2048,512,1,1]{1,0,3,2:T(8,128)S(1)} %fusion.16, bf16[16,2,64,2048]{3,2,1,0:T(8,128)(2,1)} %get-tuple-element.11, bf16[16,2,64,512]{3,2,1,0:T(8,128)(2,1)} %collective-permute-done), kind=kOutput, calls=%fused_computation.6 | convolution fusion | flops 4296015872 | bytes 18874368 | tf_op jit(solution)/shard_map/nsrd,nsrv->dv/dot_general | solution.py:364
  (8 shorter events, 0.1 us)
Async XLA Ops:
  159.3 58.4 %collective-permute-start = (bf16[16,2,64,512]{3,2,1,0:T(8,128)(2,1)S(1)}, bf16[16,2,64,512]{3,2,1,0:T(8,128)(2,1)}, u32[]{:S(2)}, u32[]{:S(2)}) collective-permute-start(bf16[16,2,64,512]{3,2,1,0:T(8,128)(2,1)S(1)} %fusion.3), channel_id=1, source_target_pairs={{0,1},{1,0},{2,3},{3,2},{4,5},{5,4},{6,7},{7,6},{8,9},{9,8},{10,11... | collective-permute-start | bytes 6291464 | tf_op jit(solution)/shard_map/ppermute | solution.py:359
